TPU v7x, 32 devices: a whole 2x2x4 slice. The times are simulated.
32 devices in a mesh: track: 8 (over z, x), lane: 4 (over y, core).
Axes of the slice: x: 2, y: 2, z: 4, core: 2. Of those that a mesh axis runs over, the one named last changes fastest.
Arguments:
- signal: float32 [8, 4, 4096, 512], P('track', 'lane'), may hold values from -8 to 8, as said below
- tap_gain: float32 [3, 512], replicated, may hold values from 0.3 to 1.2
Outputs:
- filtered: float32 [8, 4, 4096, 512], P('track', 'lane')
Inputs may be any that keep to these rules, and one draw needn't show every extreme that they name: signal holds numbers from -8 to 8.
All inputs are finite; a program needn't handle non-finite values.
Results may differ from a plain program's by a relative error of at most 0.0003.
Values sent between devices are 32-bit elements.
A program may use at most 64 MiB of HBM per device.

v0:
```python
import jax
import jax.numpy as jnp
from jax import lax
from jax.sharding import PartitionSpec as P


def passed_along(block, axis, distance):
    devices = range(lax.axis_size(axis))
    route = [((i - distance) % len(devices), i) for i in devices]
    return lax.ppermute(block, axis, route)


def local(signal, tap_gain):
    wide_in = signal.astype(jnp.float32)
    copy_1 = passed_along(signal, "track", 1)
    copy_2 = passed_along(signal, "track", 2)
    mixed = (
        tap_gain[0] * wide_in
        + tap_gain[1] * copy_1.astype(jnp.float32)
        + tap_gain[2] * copy_2.astype(jnp.float32)
    )
    filtered = jnp.tanh(mixed).astype(jnp.float32)
    return filtered


def solution(mesh):
    in_specs = (P("track", "lane", None, None), P())
    out_specs = P("track", "lane", None, None)
    return jax.shard_map(local, mesh=mesh, in_specs=in_specs, out_specs=out_specs, check_vma=False)
```

profile of v0, /device:TPU:0, one launch (start us, length us, event | category | flops | bytes accessed | tf_op | source)
XLA Modules:
  0.0 374.1 jit_solution(13401989396921606165)
XLA Ops:
  0.0 3.1 collective-permute-start.1
  3.1 1.5 collective-permute-start
  4.6 0.8 fusion
  5.4 180.8 %collective-permute-done.1 = f32[1,1,4096,512]{3,2,1,0:T(8,128)S(1)} collective-permute-done((f32[1,1,4096,512]{3,2,1,0:T(8,128)}, f32[1,1,4096,512]{3,2,1,0:T(8,128)S(1)}, u32[]{:S(2)}, u32[]{:S(2)}) %collective-permute-start.1) | collective-permute-done | bytes 8388640 | tf_op jit(solution)/shard_map/ppermute | solution.py:10
  186.2 180.9 %collective-permute-done = f32[1,1,4096,512]{3,2,1,0:T(8,128)S(1)} collective-permute-done((f32[1,1,4096,512]{3,2,1,0:T(8,128)}, f32[1,1,4096,512]{3,2,1,0:T(8,128)S(1)}, u32[]{:S(2)}, u32[]{:S(2)}) %collective-permute-start) | collective-permute-done | bytes 8388640 | tf_op jit(solution)/shard_map/ppermute | solution.py:10
  367.1 7.0 %add_tanh_fusion = f32[1,1,4096,512]{3,2,1,0:T(8,128)} fusion(f32[1,1,4096,512]{3,2,1,0:T(8,128)S(1)} %collective-permute-done.1, f32[1,1,4096,512]{3,2,1,0:T(8,128)S(1)} %collective-permute-done, f32[1,1,4096,512]{3,2,1,0:T(8,128)} %param.2, f32[512]{0:T(512)S(1)} %bitcast.4, f32[512]{0:T(512)S(1)} %bitcast.5, f32[512]{0:T(512)S(1)} %bitcast.3), kind=kLoop, calls=%fused_computation | loop fusion | flops 10485760 | bytes 33560576 | tf_op jit(solution)/shard_map/tanh | solution.py:22
Async XLA Ops:
  0.0 186.2 %collective-permute-start.1 = (f32[1,1,4096,512]{3,2,1,0:T(8,128)}, f32[1,1,4096,512]{3,2,1,0:T(8,128)S(1)}, u32[]{:S(2)}, u32[]{:S(2)}) collective-permute-start(f32[1,1,4096,512]{3,2,1,0:T(8,128)} %param.2), channel_id=1, source_target_pairs={{24,0},{28,4},{0,8},{4,12},{8,16},{12,20},{16,24},{20,28},{25,1},{... | collective-permute-start | bytes 25165832 | tf_op jit(solution)/shard_map/ppermute | solution.py:10
  3.1 364.1 %collective-permute-start = (f32[1,1,4096,512]{3,2,1,0:T(8,128)}, f32[1,1,4096,512]{3,2,1,0:T(8,128)S(1)}, u32[]{:S(2)}, u32[]{:S(2)}) collective-permute-start(f32[1,1,4096,512]{3,2,1,0:T(8,128)} %param.2), channel_id=1, source_target_pairs={{28,0},{0,4},{4,8},{8,12},{12,16},{16,20},{20,24},{24,28},{29,1},{... | collective-permute-start | bytes 25165832 | tf_op jit(solution)/shard_map/ppermute | solution.py:10
where the time goes:
time: 374 us
  waiting for transfers between devices  362 us (97%)
  other arithmetic  6.95 us (2%)
  starting transfers between devices  4.58 us (1%)
    ppermute x2, waiting for transfers between devices, passed_along(): return lax.ppermute(block, axis, route)  362 us
  transfers between devices with their start and end apart: 2, of which 2 were waited for; matrix products, arithmetic and copies ran while one was open for 0% of the time, Pallas kernels for 0%

commit v1 on v0

v1 whole, which is shorter than its diff:
```python
import functools

import jax
import jax.numpy as jnp
from jax import lax
from jax.experimental import pallas as pl
from jax.experimental.pallas import tpu as pltpu
from jax.sharding import PartitionSpec as P

CHUNKS = 64
AHEAD = 6
BAND = 32


def kernel(n, chunks, signal, gain, out, own, far, near, local_sem, send_sem, far_sem, near_sem):
    me = lax.axis_index("track")
    odd = lax.rem(me, 2)
    partner = me + 1 - 2 * odd
    after, before = lax.rem(me + 2, n), lax.rem(me + n - 2, n)
    steps = signal.shape[0]
    rows = steps // chunks

    def part(ref, k):
        return ref.at[pl.ds(pl.multiple_of(k * rows, rows), rows)]

    def to_after(k):
        return pltpu.make_async_remote_copy(
            part(signal, k), part(far, k), send_sem.at[0], far_sem.at[k],
            device_id={"track": after}, device_id_type=pl.DeviceIdType.MESH)

    def to_partner(source, k):
        return pltpu.make_async_remote_copy(
            part(source, k), part(near, k), send_sem.at[1], near_sem.at[k],
            device_id={"track": partner}, device_id_type=pl.DeviceIdType.MESH)

    def send(k):
        to_after(k).start()

        @pl.when(odd == 0)
        def _():
            to_partner(signal, k).start()

    load = pltpu.make_async_copy(signal, own, local_sem)
    load.start()

    barrier = pltpu.get_barrier_semaphore()
    for other in (partner, after, before):
        pl.semaphore_signal(barrier, inc=1, device_id={"track": other}, device_id_type=pl.DeviceIdType.MESH)
    pl.semaphore_wait(barrier, 3)

    @pl.loop(0, min(AHEAD, chunks))
    def _(k):
        send(k)

    load.wait()

    def mix(k):
        to_partner(signal, k).wait_recv()


        @pl.loop(0, rows // BAND)
        def _(b):
            at = pl.ds(pl.multiple_of(k * rows + b * BAND, BAND), BAND)
            out[at] = jnp.tanh(gain[0:1] * own[at] + gain[1:2] * near[at] + gain[2:3] * far[at])

    @pl.loop(0, chunks)
    def _(k):
        to_after(k).wait_recv()

        @pl.when(odd == 1)
        def _():
            to_partner(far, k).start()

        @pl.when(k + AHEAD < chunks)
        def _():
            send(k + AHEAD)

        @pl.when(k > 0)
        def _():
            mix(k - 1)

    mix(chunks - 1)
    pltpu.make_async_remote_copy(
        signal, far, send_sem.at[0], far_sem.at[0],
        device_id={"track": after}, device_id_type=pl.DeviceIdType.MESH).wait_send()
    pltpu.make_async_remote_copy(
        signal, near, send_sem.at[1], near_sem.at[0],
        device_id={"track": partner}, device_id_type=pl.DeviceIdType.MESH).wait_send()


def solution(mesh):
    n = mesh.shape["track"]

    def local(signal, tap_gain):
        steps, channels = signal.shape[-2:]
        block = (steps, channels)
        out = pl.pallas_call(
            functools.partial(kernel, n, CHUNKS),
            out_shape=pltpu.VMEM(block, jnp.float32),
            in_specs=[pl.BlockSpec(memory_space=pltpu.HBM), pl.BlockSpec(memory_space=pltpu.VMEM)],
            out_specs=pl.BlockSpec(memory_space=pltpu.VMEM),
            scratch_shapes=[
                pltpu.VMEM(block, jnp.float32),
                pltpu.VMEM(block, jnp.float32),
                pltpu.VMEM(block, jnp.float32),
                pltpu.SemaphoreType.DMA,
                pltpu.SemaphoreType.DMA((2,)),
                pltpu.SemaphoreType.DMA((CHUNKS,)),
                pltpu.SemaphoreType.DMA((CHUNKS,)),
            ],
            compiler_params=pltpu.CompilerParams(
                collective_id=0, has_side_effects=True, vmem_limit_bytes=48 * 1024 * 1024),
        )(signal.reshape(block), tap_gain)
        return out.reshape(signal.shape)

    in_specs = (P("track", "lane", None, None), P())
    out_specs = P("track", "lane", None, None)
    return jax.shard_map(local, mesh=mesh, in_specs=in_specs, out_specs=out_specs, check_vma=False)
```

time: 374 us -> 197 us (0.53)
  waiting for transfers between devices: 362 us -> 0 us
  Pallas kernels: 0 us -> 193 us
  other arithmetic: 6.95 us -> 0 us
  starting transfers between devices: 4.58 us -> 0 us
    ppermute x2 -> x0, waiting for transfers between devices: 362 us -> none  [passed_along(): return lax.ppermute(block, axis, route)]
    pallas_call x0 -> x1, Pallas kernels: none -> 193 us  [local(): pl.pallas_call(functools.partial(kernel, n, CHUNKS), out_shape=pltpu.VMEM...]
    tanh x1 -> x0, other arithmetic: 6.95 us -> none  [local(): filtered = jnp.tanh(mixed).astype(jnp.float32)]
    ppermute x2 -> x0, starting transfers between devices: 4.58 us -> none  [passed_along(): return lax.ppermute(block, axis, route)]
  transfers between devices with their start and end apart: 2 -> 0, of which waited for: 2 -> 0; matrix products, arithmetic and copies ran while one was open for 0% -> 0% of each run, Pallas kernels for 0% -> 0%
where the time goes in v1:
time: 197 us
  Pallas kernels  193 us (98%)
  local copies, waits for them, and re-layouts  3.4 us (2%)
    pallas_call x1, Pallas kernels, local(): pl.pallas_call(functools.partial(kernel, n, CHUNKS), out_shape=pltpu.VMEM...  193 us

profile of v1, /device:TPU:0, one launch (start us, length us, event | category | flops | bytes accessed | tf_op | source)
XLA Modules:
  0.0 196.9 jit_solution(13628894996862262295)
XLA Ops:
  0.0 193.5 %shard_map.28 = f32[4096,512]{1,0:T(8,128)S(1)} custom-call(f32[4096,512]{1,0:T(8,128)} %bitcast.3, f32[3,512]{1,0:T(4,128)} %gain.1), custom_call_target="tpu_custom_call" | custom-call | tf_op jit(solution)/shard_map/pallas_call | solution.py:97
  193.5 3.4 %copy.4 = f32[1,1,4096,512]{3,2,1,0:T(8,128)} copy(f32[1,1,4096,512]{3,2,1,0:T(8,128)S(1)} %bitcast.2) | data formatting | bytes 16777216

commit v2 on v1

v2 whole, which is shorter than its diff:
```python
import functools

import jax
import jax.numpy as jnp
from jax import lax
from jax.experimental import pallas as pl
from jax.experimental.pallas import tpu as pltpu
from jax.sharding import PartitionSpec as P

CHUNKS = 32
EARLY = 2
AHEAD = 4
BAND = 32
LOGICAL = pl.DeviceIdType.MESH


def kernel(n, signal, gain, out, own, far, near, blend, load_sem, send_sem, far_sem, near_sem):
    me = lax.axis_index("track")
    odd = lax.rem(me, 2)
    partner = me + 1 - 2 * odd
    after, before = lax.rem(me + 2, n), lax.rem(me + n - 2, n)
    rows = signal.shape[0] // CHUNKS
    relayed = CHUNKS - EARLY

    def span(k, count=1):
        start = k * rows if isinstance(k, int) else pl.multiple_of(k * rows, rows)
        return pl.ds(start, count * rows)

    def to_after(source, dest):
        return lambda k: pltpu.make_async_remote_copy(
            source, far.at[dest], send_sem.at[0], far_sem.at[k],
            device_id={"track": after}, device_id_type=LOGICAL)

    def to_partner(source, dest):
        return lambda k: pltpu.make_async_remote_copy(
            source, near.at[dest], send_sem.at[1], near_sem.at[k],
            device_id={"track": partner}, device_id_type=LOGICAL)

    def wait_far(k):
        to_after(own.at[span(k)], span(k))(k).wait_recv()

    def wait_near(k):
        to_partner(own.at[span(k)], span(k))(k).wait_recv()

    def send(k):
        plain = jnp.logical_or(odd == 1, k < relayed)

        @pl.when(plain)
        def _():
            to_after(own.at[span(k)], span(k))(k).start()

        @pl.when(jnp.logical_not(plain))
        def _():
            to_after(blend.at[span(k - relayed)], span(k))(k).start()

        @pl.when(odd == 0)
        def _():
            to_partner(own.at[span(k)], span(k))(k).start()

    def bands(k, body):
        @pl.loop(0, rows // BAND)
        def _(b):
            body(pl.ds(pl.multiple_of(k * rows + b * BAND, BAND), BAND))

    def mix(k):
        wait_near(k)

        def body(at):
            out[at] = jnp.tanh(gain[0:1] * own[at] + gain[1:2] * near[at] + gain[2:3] * far[at])

        bands(k, body)

    def mix_blended(k):
        def body(at):
            out[at] = jnp.tanh(gain[0:1] * own[at] + far[at])

        bands(k, body)

    head = pltpu.make_async_copy(signal.at[span(0, AHEAD)], own.at[span(0, AHEAD)], load_sem.at[0])
    rest = pltpu.make_async_copy(
        signal.at[span(AHEAD, CHUNKS - AHEAD)], own.at[span(AHEAD, CHUNKS - AHEAD)], load_sem.at[1])
    head.start()
    rest.start()

    barrier = pltpu.get_barrier_semaphore()
    for other in (partner, before):
        pl.semaphore_signal(barrier, inc=1, device_id={"track": other}, device_id_type=LOGICAL)
    pl.semaphore_wait(barrier, 2)

    @pl.when(odd == 1)
    def _():
        @pl.loop(relayed, CHUNKS)
        def _(k):
            to_partner(signal.at[span(k)], span(k))(k).start()

    head.wait()

    @pl.loop(0, AHEAD)
    def _(k):
        send(k)

    rest.wait()

    def step(k):
        wait_far(k)

        @pl.when(jnp.logical_and(odd == 1, k < relayed))
        def _():
            to_partner(far.at[span(k)], span(k))(k).start()

        @pl.when(k + AHEAD < CHUNKS)
        def _():
            send(k + AHEAD)

        @pl.when(jnp.logical_and(odd == 1, k > 0))
        def _():
            mix(k - 1)

        @pl.when(jnp.logical_and(odd == 0, k > relayed))
        def _():
            mix_blended(k - 1)

        @pl.when(jnp.logical_and(odd == 0, k >= EARLY))
        def _():
            mix(k - EARLY)

    pl.loop(0, CHUNKS // 2)(step)

    @pl.when(odd == 0)
    def _():
        @pl.loop(relayed, CHUNKS)
        def _(k):
            wait_near(k)

            @pl.loop(0, rows // BAND)
            def _(b):
                at = pl.ds(pl.multiple_of(k * rows + b * BAND, BAND), BAND)
                to = pl.ds(pl.multiple_of((k - relayed) * rows + b * BAND, BAND), BAND)
                blend[to] = gain[1:2] * near[at] + gain[2:3] * own[at]

    pl.loop(CHUNKS // 2, CHUNKS)(step)

    @pl.when(odd == 1)
    def _():
        mix(CHUNKS - 1)

    @pl.when(odd == 0)
    def _():
        mix_blended(CHUNKS - 1)

    to_after(own, span(0, CHUNKS))(0).wait_send()
    to_partner(own, span(0, CHUNKS))(0).wait_send()


def solution(mesh):
    n = mesh.shape["track"]

    def local(signal, tap_gain):
        steps, channels = signal.shape[-2:]
        block = (steps, channels)
        out = pl.pallas_call(
            functools.partial(kernel, n),
            out_shape=pltpu.VMEM(block, jnp.float32),
            in_specs=[pl.BlockSpec(memory_space=pltpu.HBM), pl.BlockSpec(memory_space=pltpu.VMEM)],
            out_specs=pl.BlockSpec(memory_space=pltpu.VMEM),
            scratch_shapes=[
                pltpu.VMEM(block, jnp.float32),
                pltpu.VMEM(block, jnp.float32),
                pltpu.VMEM(block, jnp.float32),
                pltpu.VMEM((steps // CHUNKS * EARLY, channels), jnp.float32),
                pltpu.SemaphoreType.DMA((2,)),
                pltpu.SemaphoreType.DMA((2,)),
                pltpu.SemaphoreType.DMA((CHUNKS,)),
                pltpu.SemaphoreType.DMA((CHUNKS,)),
            ],
            compiler_params=pltpu.CompilerParams(
                collective_id=0, has_side_effects=True, vmem_limit_bytes=48 * 1024 * 1024),
        )(signal.reshape(block), tap_gain)
        return out.reshape(signal.shape)

    in_specs = (P("track", "lane", None, None), P())
    out_specs = P("track", "lane", None, None)
    return jax.shard_map(local, mesh=mesh, in_specs=in_specs, out_specs=out_specs, check_vma=False)
```

time: 197 us -> 192 us (0.975)
  Pallas kernels: 193 us -> 189 us
    pallas_call x1, Pallas kernels: 193 us -> 189 us  [local(): pl.pallas_call(functools.partial(kernel, n), out_shape=pltpu.VMEM(block,...]
where the time goes in v2:
time: 192 us
  Pallas kernels  189 us (98%)
  local copies, waits for them, and re-layouts  3.4 us (2%)
    pallas_call x1, Pallas kernels, local(): pl.pallas_call(functools.partial(kernel, n), out_shape=pltpu.VMEM(block,...  189 us

profile of v2, /device:TPU:0, one launch (start us, length us, event | category | flops | bytes accessed | tf_op | source)
XLA Modules:
  0.0 192.2 jit_solution(6235837091372538410)
XLA Ops:
  0.0 188.8 %shard_map.28 = f32[4096,512]{1,0:T(8,128)S(1)} custom-call(f32[4096,512]{1,0:T(8,128)} %bitcast.3, f32[3,512]{1,0:T(4,128)} %gain.1), custom_call_target="tpu_custom_call" | custom-call | tf_op jit(solution)/shard_map/pallas_call | solution.py:161
  188.8 3.4 %copy.4 = f32[1,1,4096,512]{3,2,1,0:T(8,128)} copy(f32[1,1,4096,512]{3,2,1,0:T(8,128)S(1)} %bitcast.2) | data formatting | bytes 16777216

commit v3 on v2

--- a/solution.py
+++ b/solution.py
@@ -11,6 +11,7 @@
 EARLY = 2
 AHEAD = 4
 BAND = 32
+TAIL = 4
 LOGICAL = pl.DeviceIdType.MESH
 
 
@@ -21,6 +22,7 @@
     after, before = lax.rem(me + 2, n), lax.rem(me + n - 2, n)
     rows = signal.shape[0] // CHUNKS
     relayed = CHUNKS - EARLY
+    last = CHUNKS - 1
 
     def span(k, count=1):
         start = k * rows if isinstance(k, int) else pl.multiple_of(k * rows, rows)
@@ -57,6 +59,26 @@
         def _():
             to_partner(own.at[span(k)], span(k))(k).start()
 
+    def piece(j, base=last):
+        return pl.ds(base * rows + j * (rows // TAIL), rows // TAIL)
+
+    def send_tail():
+        for j in range(TAIL):
+            @pl.when(odd == 1)
+            def _():
+                to_after(own.at[piece(j)], piece(j))(last + j).start()
+
+            @pl.when(odd == 0)
+            def _():
+                to_after(blend.at[piece(j, last - relayed)], piece(j))(last + j).start()
+                to_partner(own.at[piece(j)], piece(j))(last + j).start()
+
+    def band(at):
+        out[at] = jnp.tanh(gain[0:1] * own[at] + gain[1:2] * near[at] + gain[2:3] * far[at])
+
+    def band_blended(at):
+        out[at] = jnp.tanh(gain[0:1] * own[at] + far[at])
+
     def bands(k, body):
         @pl.loop(0, rows // BAND)
         def _(b):
@@ -64,21 +86,26 @@
 
     def mix(k):
         wait_near(k)
-
-        def body(at):
-            out[at] = jnp.tanh(gain[0:1] * own[at] + gain[1:2] * near[at] + gain[2:3] * far[at])
-
-        bands(k, body)
+        bands(k, band)
 
     def mix_blended(k):
-        def body(at):
-            out[at] = jnp.tanh(gain[0:1] * own[at] + far[at])
-
-        bands(k, body)
-
-    head = pltpu.make_async_copy(signal.at[span(0, AHEAD)], own.at[span(0, AHEAD)], load_sem.at[0])
+        bands(k, band_blended)
+
+    def mix_piece(j):
+        to_after(own.at[piece(j)], piece(j))(last + j).wait_recv()
+
+        @pl.when(odd == 1)
+        def _():
+            to_partner(own.at[piece(j)], piece(j))(last + j).wait_recv()
+            band(piece(j))
+
+        @pl.when(odd == 0)
+        def _():
+            band_blended(piece(j))
+
+    head = pltpu.make_async_copy(signal.at[span(0)], own.at[span(0)], load_sem.at[0])
     rest = pltpu.make_async_copy(
-        signal.at[span(AHEAD, CHUNKS - AHEAD)], own.at[span(AHEAD, CHUNKS - AHEAD)], load_sem.at[1])
+        signal.at[span(1, CHUNKS - 1)], own.at[span(1, CHUNKS - 1)], load_sem.at[1])
     head.start()
     rest.start()
 
@@ -94,12 +121,9 @@
             to_partner(signal.at[span(k)], span(k))(k).start()
 
     head.wait()
-
-    @pl.loop(0, AHEAD)
-    def _(k):
-        send(k)
-
+    send(0)
     rest.wait()
+    pl.loop(1, AHEAD)(send)
 
     def step(k):
         wait_far(k)
@@ -108,9 +132,13 @@
         def _():
             to_partner(far.at[span(k)], span(k))(k).start()
 
-        @pl.when(k + AHEAD < CHUNKS)
+        @pl.when(k + AHEAD < last)
         def _():
             send(k + AHEAD)
+
+        @pl.when(k + AHEAD == last)
+        def _():
+            send_tail()
 
         @pl.when(jnp.logical_and(odd == 1, k > 0))
         def _():
@@ -138,15 +166,24 @@
                 to = pl.ds(pl.multiple_of((k - relayed) * rows + b * BAND, BAND), BAND)
                 blend[to] = gain[1:2] * near[at] + gain[2:3] * own[at]
 
-    pl.loop(CHUNKS // 2, CHUNKS)(step)
+    pl.loop(CHUNKS // 2, last)(step)
 
     @pl.when(odd == 1)
     def _():
-        mix(CHUNKS - 1)
+        mix(last - 1)
 
     @pl.when(odd == 0)
     def _():
-        mix_blended(CHUNKS - 1)
+        mix_blended(last - 1)
+
+    for j in range(TAIL - 1):
+        mix_piece(j)
+
+    @pl.when(odd == 0)
+    def _():
+        mix(relayed - 1)
+
+    mix_piece(TAIL - 1)
 
     to_after(own, span(0, CHUNKS))(0).wait_send()
     to_partner(own, span(0, CHUNKS))(0).wait_send()
@@ -170,8 +207,8 @@
                 pltpu.VMEM((steps // CHUNKS * EARLY, channels), jnp.float32),
                 pltpu.SemaphoreType.DMA((2,)),
                 pltpu.SemaphoreType.DMA((2,)),
-                pltpu.SemaphoreType.DMA((CHUNKS,)),
-                pltpu.SemaphoreType.DMA((CHUNKS,)),
+                pltpu.SemaphoreType.DMA((CHUNKS - 1 + TAIL,)),
+                pltpu.SemaphoreType.DMA((CHUNKS - 1 + TAIL,)),
             ],
             compiler_params=pltpu.CompilerParams(
                 collective_id=0, has_side_effects=True, vmem_limit_bytes=48 * 1024 * 1024),

time: 192 us -> 192 us (level)
  no operation moved by 1% of the time
where the time goes in v3:
time: 192 us
  Pallas kernels  189 us (98%)
  local copies, waits for them, and re-layouts  3.4 us (2%)
    pallas_call x1, Pallas kernels, local(): pl.pallas_call(functools.partial(kernel, n), out_shape=pltpu.VMEM(block,...  189 us

profile of v3, /device:TPU:0, one launch (start us, length us, event | category | flops | bytes accessed | tf_op | source)
XLA Modules:
  0.0 192.0 jit_solution(1150745375545997677)
XLA Ops:
  0.0 188.6 %shard_map.28 = f32[4096,512]{1,0:T(8,128)S(1)} custom-call(f32[4096,512]{1,0:T(8,128)} %bitcast.3, f32[3,512]{1,0:T(4,128)} %gain.1), custom_call_target="tpu_custom_call" | custom-call | tf_op jit(solution)/shard_map/pallas_call | solution.py:198
  188.6 3.4 %copy.4 = f32[1,1,4096,512]{3,2,1,0:T(8,128)} copy(f32[1,1,4096,512]{3,2,1,0:T(8,128)S(1)} %bitcast.2) | data formatting | bytes 16777216
